TPU v7x, 32 devices: a whole 2x2x4 slice. The times are simulated.
32 devices in a mesh: blk: 16 (over z, x, core), cat: 2 (over y).
Axes of the slice: x: 2, y: 2, z: 4, core: 2. Of those that a mesh axis runs over, the one named last changes fastest.
Arguments:
- item_content: bfloat16 [32768, 512], P('blk', 'cat'), may hold values from -6 to 6
- projection: bfloat16 [512, 256], replicated, may hold values from -0.06591797 to 0.06591797
- send_order: int32 [32, 1024], P(('blk', 'cat')), may hold values from 0 to 1023, each once within a row
- user_factors: float32 [16384, 256], P(('blk', 'cat')), may hold values from -1.5 to 1.5
- ratings: int32 [16384, 4, 1024], P(('blk', 'cat')), may hold values from 0 to 5, as said below
Outputs:
- users_out: float32 [16384, 256], P(('blk', 'cat'))
- items_out: float32 [32768, 256], P(('blk', 'cat'))
Inputs may be any that keep to these rules, and one draw needn't show every extreme that they name: `send_order`: each row is a permutation of 0 .. 1023. `ratings`: 0 means no rating, 1 to 5 a rating.
All inputs are finite; a program needn't handle non-finite values.
Results may differ from a plain program's by a relative error of at most 0.0003.
Values may be sent and summed in bfloat16 or wider, within the bound.
A program may use at most 64 MiB of HBM per device.

v0:
```python
import jax
import jax.numpy as jnp
from jax import lax
from jax.sharding import PartitionSpec as P

ROUNDS = 4


learn_rate = 0.004
shrink = 0.05


def passed_along(shard, axis, by):
    size = lax.axis_size(axis)
    return lax.ppermute(shard, axis, [(i, (i + by) % size) for i in range(size)])


def update(users, items, values):
    masks = jnp.where(values > 0, jnp.float32(1.0), jnp.float32(0.0))
    guess = lax.dot_general(users, items, (((1,), (1,)), ((), ())), precision=lax.Precision.HIGHEST)
    errors = masks * (values - guess)
    user_grad = jnp.dot(errors, items, precision=lax.Precision.HIGHEST)
    item_grad = lax.dot_general(
        errors, users, (((0,), (0,)), ((), ())), precision=lax.Precision.HIGHEST
    )
    return (
        users + learn_rate * (user_grad - shrink * users),
        items + learn_rate * (item_grad - shrink * items),
    )


def body(item_content, projection, send_order, user_factors, ratings):
    own_rows = lax.all_to_all(item_content, "cat", split_axis=0, concat_axis=1, tiled=True)
    owned = jnp.dot(own_rows, projection, preferred_element_type=jnp.float32)
    users = user_factors
    deal_order = send_order[0]
    ordered = jnp.take(owned, deal_order, axis=0)
    items = lax.all_to_all(ordered, "blk", split_axis=0, concat_axis=0, tiled=True)
    for round_index in range(ROUNDS):
        if round_index > 0:
            items = passed_along(items, "blk", 1)
        values = ratings[:, round_index, :].astype(jnp.float32)
        users, items = update(users, items, values)
    return (users, items)


def solution(mesh):
    placed = (
        P("blk", "cat"),
        P(),
        P(("blk", "cat"), None),
        P(("blk", "cat"), None),
        P(("blk", "cat"), None, None),
    )
    return jax.shard_map(
        body,
        mesh=mesh,
        in_specs=placed,
        out_specs=(P(("blk", "cat"), None), P(("blk", "cat"), None)),
        check_vma=False,
    )
```

profile of v0, /device:TPU:0, one launch (start us, length us, event | category | flops | bytes accessed | tf_op | source)
XLA Modules:
  0.0 139.1 jit_solution(2077380146038367120)
XLA Ops:
  0.6 0.0 copy-start
  0.7 4.4 %all-to-all-start = ((bf16[2,1024,256]{2,1,0:T(8,128)(2,1)}), bf16[2,1024,256]{2,1,0:T(8,128)(2,1)S(1)}, u32[]{:S(2)}, u32[]{:S(2)}) async-start(bf16[2,1024,256]{2,1,0:T(8,128)(2,1)} %bitcast.70), calls=%async_computation | async-start | bytes 2097152 | tf_op jit(solution)/shard_map/all_to_all | solution.py:33
  5.1 0.5 broadcast.78
  5.6 0.7 reduce.3
  6.3 0.1 squeeze.4
  6.3 13.2 %all-to-all-done = bf16[2,1024,256]{2,1,0:T(8,128)(2,1)S(1)} async-done(((bf16[2,1024,256]{2,1,0:T(8,128)(2,1)}), bf16[2,1024,256]{2,1,0:T(8,128)(2,1)S(1)}, u32[]{:S(2)}, u32[]{:S(2)}) %all-to-all-start) | async-done | bytes 1048608 | tf_op jit(solution)/shard_map/all_to_all | solution.py:33
  19.5 0.5 copy.22
  20.0 0.5 fusion.15
  20.5 3.5 %gather_fusion = f32[1024,256]{1,0:T(8,128)S(1)} fusion(f32[1024,256]{1,0:T(8,128)S(1)} %fusion.15, s32[1024]{0:T(1024)S(1)} %broadcast_clamp_fusion), kind=kCustom, calls=%fused_computation | custom fusion | bytes 2101248 | tf_op jit(solution)/shard_map/jit(_take)/gather | solution.py:37
  24.0 1.2 broadcast_select_fusion
  25.2 6.1 %all-to-all-start.1 = ((f32[16,64,256]{2,1,0:T(8,128)}), f32[16,64,256]{2,1,0:T(8,128)S(1)}, u32[]{:S(2)}, u32[]{:S(2)}) async-start(f32[16,64,256]{2,1,0:T(8,128)} %broadcast_select_fusion), calls=%async_computation.1 | async-start | bytes 2097152 | tf_op jit(solution)/shard_map/all_to_all | solution.py:38
  31.3 19.8 %fusion.14 = (s32[512,1,1024]{2,1,0:T(1,128)}, s32[512,1,1024]{2,1,0:T(1,128)}, s32[512,1,1024]{2,1,0:T(1,128)}, s32[512,1,1024]{2,1,0:T(1,128)S(1)}) fusion(s32[512,4,1024]{2,1,0:T(4,128)} %param.9), kind=kLoop, calls=%fused_computation.36 | loop fusion | bytes 16777216 | tf_op jit(solution)/shard_map/slice | solution.py:42
  51.1 4.4 %copy.32 = s32[512,1,1024]{0,2,1:T(8,128)} copy(s32[512,1,1024]{2,1,0:T(1,128)S(1)} %get-tuple-element.5) | data formatting | bytes 4194304
  55.6 3.9 %fusion.3 = f32[512,1024]{0,1:T(8,128)S(1)} fusion(s32[512,1,1024]{0,2,1:T(8,128)} %copy.32, f32[1024,256]{1,0:T(8,128)S(1)} %bitcast.64, f32[512,256]{1,0:T(8,128)} %param.8), kind=kOutput, calls=%fused_computation.11 | convolution fusion | flops 1613234176 | bytes 5767168 | tf_op jit(solution)/shard_map/dot_general | solution.py:20
  59.5 2.8 %fusion.5 = f32[1024,256]{1,0:T(8,128)} fusion(f32[1024,256]{1,0:T(8,128)S(1)} %bitcast.65, f32[512,1024]{0,1:T(8,128)S(1)} %fusion.3, f32[512,256]{1,0:T(8,128)S(1)} %copy-done.6), kind=kOutput, calls=%fused_computation.15 | convolution fusion | flops 1611661312 | bytes 4718592 | tf_op jit(solution)/shard_map/dot_general | solution.py:23
  62.2 0.4 collective-permute-start
  62.6 6.0 %copy.33 = s32[512,1,1024]{0,2,1:T(8,128)} copy(s32[512,1,1024]{2,1,0:T(1,128)} %get-tuple-element.4) | data formatting | bytes 4194304
  68.7 4.6 %fusion.10 = f32[512,256]{1,0:T(8,128)S(1)} fusion(f32[512,256]{1,0:T(8,128)} %param.8, f32[512,1024]{0,1:T(8,128)S(1)} %fusion.3, f32[1024,256]{1,0:T(8,128)S(1)} %bitcast.66), kind=kOutput, calls=%fused_computation.24 | convolution fusion | flops 1611137024 | bytes 4194304 | tf_op jit(solution)/shard_map/dot_general | solution.py:22
  73.4 6.1 %collective-permute-done = f32[1024,256]{1,0:T(8,128)} collective-permute-done((f32[1024,256]{1,0:T(8,128)}, f32[1024,256]{1,0:T(8,128)}, u32[]{:S(2)}, u32[]{:S(2)}) %collective-permute-start) | collective-permute-done | bytes 1048608 | tf_op jit(solution)/shard_map/ppermute | solution.py:15
  79.5 3.4 %fusion.2 = f32[512,1024]{0,1:T(8,128)S(1)} fusion(s32[512,1,1024]{0,2,1:T(8,128)S(1)} %copy-done.3, f32[512,256]{1,0:T(8,128)S(1)} %fusion.10, f32[1024,256]{1,0:T(8,128)} %collective-permute-done), kind=kOutput, calls=%fused_computation.9 | convolution fusion | flops 1613234176 | bytes 5767168 | tf_op jit(solution)/shard_map/dot_general | solution.py:20
  82.9 4.0 %multiply_add_fusion.2 = f32[1024,256]{1,0:T(8,128)} fusion(f32[1024,256]{1,0:T(8,128)} %collective-permute-done, f32[512,1024]{0,1:T(8,128)S(1)} %fusion.2, f32[512,256]{1,0:T(8,128)S(1)} %fusion.10), kind=kOutput, calls=%fused_computation.30 | convolution fusion | flops 1611661312 | bytes 4718592 | tf_op jit(solution)/shard_map/dot_general | solution.py:23
  86.9 6.0 %copy.34 = s32[512,1,1024]{0,2,1:T(8,128)} copy(s32[512,1,1024]{2,1,0:T(1,128)} %get-tuple-element.3) | data formatting | bytes 4194304
  92.9 5.0 %fusion.11 = f32[512,256]{1,0:T(8,128)S(1)} fusion(f32[512,256]{1,0:T(8,128)} %copy-done.5, f32[512,1024]{0,1:T(8,128)S(1)} %fusion.2, f32[1024,256]{1,0:T(8,128)} %collective-permute-done), kind=kOutput, calls=%fused_computation.25 | convolution fusion | flops 1611137024 | bytes 4194304 | tf_op jit(solution)/shard_map/dot_general | solution.py:22
  97.9 6.1 %collective-permute-done.1 = f32[1024,256]{1,0:T(8,128)S(1)} collective-permute-done((f32[1024,256]{1,0:T(8,128)}, f32[1024,256]{1,0:T(8,128)S(1)}, u32[]{:S(2)}, u32[]{:S(2)}) %collective-permute-start.1) | collective-permute-done | bytes 1048608 | tf_op jit(solution)/shard_map/ppermute | solution.py:15
  104.0 2.1 %fusion.1 = f32[512,1024]{0,1:T(8,128)S(1)} fusion(s32[512,1,1024]{0,2,1:T(8,128)S(1)} %copy-done.1, f32[512,256]{1,0:T(8,128)S(1)} %fusion.11, f32[1024,256]{1,0:T(8,128)S(1)} %collective-permute-done.1), kind=kOutput, calls=%fused_computation.6 | convolution fusion | flops 1613234176 | bytes 5767168 | tf_op jit(solution)/shard_map/dot_general | solution.py:20
  106.1 2.8 %multiply_add_fusion.1 = f32[1024,256]{1,0:T(8,128)} fusion(f32[1024,256]{1,0:T(8,128)S(1)} %collective-permute-done.1, f32[512,1024]{0,1:T(8,128)S(1)} %fusion.1, f32[512,256]{1,0:T(8,128)S(1)} %fusion.11), kind=kOutput, calls=%fused_computation.29 | convolution fusion | flops 1611661312 | bytes 4718592 | tf_op jit(solution)/shard_map/dot_general | solution.py:23
  108.9 6.0 %copy.35 = s32[512,1,1024]{0,2,1:T(8,128)} copy(s32[512,1,1024]{2,1,0:T(1,128)} %get-tuple-element.2) | data formatting | bytes 4194304
  114.9 4.6 %fusion.12 = f32[512,256]{1,0:T(8,128)S(1)} fusion(f32[512,256]{1,0:T(8,128)} %copy-done.4, f32[512,1024]{0,1:T(8,128)S(1)} %fusion.1, f32[1024,256]{1,0:T(8,128)S(1)} %collective-permute-done.1), kind=kOutput, calls=%fused_computation.26 | convolution fusion | flops 1611137024 | bytes 4194304 | tf_op jit(solution)/shard_map/dot_general | solution.py:22
  119.6 6.6 %collective-permute-done.2 = f32[1024,256]{1,0:T(8,128)} collective-permute-done((f32[1024,256]{1,0:T(8,128)}, f32[1024,256]{1,0:T(8,128)}, u32[]{:S(2)}, u32[]{:S(2)}) %collective-permute-start.2) | collective-permute-done | bytes 1048608 | tf_op jit(solution)/shard_map/ppermute | solution.py:15
  126.2 3.4 %fusion = f32[512,1024]{0,1:T(8,128)S(1)} fusion(s32[512,1,1024]{0,2,1:T(8,128)S(1)} %copy-done.2, f32[512,256]{1,0:T(8,128)S(1)} %fusion.12, f32[1024,256]{1,0:T(8,128)} %collective-permute-done.2), kind=kOutput, calls=%fused_computation.3 | convolution fusion | flops 1613234176 | bytes 5767168 | tf_op jit(solution)/shard_map/dot_general | solution.py:20
  129.5 5.6 %fusion.13 = f32[512,256]{1,0:T(8,128)} fusion(f32[512,256]{1,0:T(8,128)S(1)} %fusion.12, f32[512,1024]{0,1:T(8,128)S(1)} %fusion, f32[1024,256]{1,0:T(8,128)} %collective-permute-done.2), kind=kOutput, calls=%fused_computation.27 | convolution fusion | flops 1611137024 | bytes 4194304 | tf_op jit(solution)/shard_map/dot_general | solution.py:22
  135.1 4.0 %multiply_add_fusion = f32[1024,256]{1,0:T(8,128)} fusion(f32[1024,256]{1,0:T(8,128)} %collective-permute-done.2, f32[512,1024]{0,1:T(8,128)S(1)} %fusion, f32[512,256]{1,0:T(8,128)S(1)} %fusion.12), kind=kOutput, calls=%fused_computation.28 | convolution fusion | flops 1611661312 | bytes 4718592 | tf_op jit(solution)/shard_map/dot_general | solution.py:23
  (21 shorter events, 0.1 us)
Async XLA Ops:
  0.6 19.4 %copy-start = (bf16[512,256]{1,0:T(8,128)(2,1)S(1)}, bf16[512,256]{1,0:T(8,128)(2,1)}, u32[]{:S(2)}) copy-start(bf16[512,256]{1,0:T(8,128)(2,1)} %param.6) | copy-start | bytes 786436
  0.6 4.4 %copy-start.7 = (s32[1,1024]{1,0:T(1,128)S(1)}, s32[1,1024]{1,0:T(1,128)}, u32[]{:S(2)}) copy-start(s32[1,1024]{1,0:T(1,128)} %param.7) | copy-start | bytes 12292
  0.7 18.8 %all-to-all-start = ((bf16[2,1024,256]{2,1,0:T(8,128)(2,1)}), bf16[2,1024,256]{2,1,0:T(8,128)(2,1)S(1)}, u32[]{:S(2)}, u32[]{:S(2)}) async-start(bf16[2,1024,256]{2,1,0:T(8,128)(2,1)} %bitcast.70), calls=%async_computation | async-start | bytes 2097152 | tf_op jit(solution)/shard_map/all_to_all | solution.py:33
  25.2 30.4 %all-to-all-start.1 = ((f32[16,64,256]{2,1,0:T(8,128)}), f32[16,64,256]{2,1,0:T(8,128)S(1)}, u32[]{:S(2)}, u32[]{:S(2)}) async-start(f32[16,64,256]{2,1,0:T(8,128)} %broadcast_select_fusion), calls=%async_computation.1 | async-start | bytes 2097152 | tf_op jit(solution)/shard_map/all_to_all | solution.py:38
  55.6 3.9 %copy-start.6 = (f32[512,256]{1,0:T(8,128)S(1)}, f32[512,256]{1,0:T(8,128)}, u32[]{:S(2)}) copy-start(f32[512,256]{1,0:T(8,128)} %param.8) | copy-start | bytes 1572868
  62.2 17.2 %collective-permute-start = (f32[1024,256]{1,0:T(8,128)}, f32[1024,256]{1,0:T(8,128)}, u32[]{:S(2)}, u32[]{:S(2)}) collective-permute-start(f32[1024,256]{1,0:T(8,128)} %fusion.5), channel_id=1, source_target_pairs={{0,2},{2,4},{4,6},{6,8},{8,10},{10,12},{12,14},{14,16},{16,18},{18... | collective-permute-start | bytes 3145736 | tf_op jit(solution)/shard_map/ppermute | solution.py:15
  68.7 10.8 %copy-start.3 = (s32[512,1,1024]{0,2,1:T(8,128)S(1)}, s32[512,1,1024]{0,2,1:T(8,128)}, u32[]{:S(2)}) copy-start(s32[512,1,1024]{0,2,1:T(8,128)} %copy.33) | copy-start | bytes 6291460
  73.3 9.5 %copy-start.5 = (f32[512,256]{1,0:T(8,128)}, f32[512,256]{1,0:T(8,128)S(1)}, u32[]{:S(2)}) copy-start(f32[512,256]{1,0:T(8,128)S(1)} %fusion.10) | copy-start | bytes 1572868
  86.9 17.1 %collective-permute-start.1 = (f32[1024,256]{1,0:T(8,128)}, f32[1024,256]{1,0:T(8,128)S(1)}, u32[]{:S(2)}, u32[]{:S(2)}) collective-permute-start(f32[1024,256]{1,0:T(8,128)} %multiply_add_fusion.2), channel_id=1, source_target_pairs={{0,2},{2,4},{4,6},{6,8},{8,10},{10,12},{12,14},{14,16},{16,18},{18... | collective-permute-start | bytes 3145736 | tf_op jit(solution)/shard_map/ppermute | solution.py:15
  92.9 11.1 %copy-start.1 = (s32[512,1,1024]{0,2,1:T(8,128)S(1)}, s32[512,1,1024]{0,2,1:T(8,128)}, u32[]{:S(2)}) copy-start(s32[512,1,1024]{0,2,1:T(8,128)} %copy.34) | copy-start | bytes 6291460
  97.9 8.3 %copy-start.4 = (f32[512,256]{1,0:T(8,128)}, f32[512,256]{1,0:T(8,128)S(1)}, u32[]{:S(2)}) copy-start(f32[512,256]{1,0:T(8,128)S(1)} %fusion.11) | copy-start | bytes 1572868
  108.9 17.2 %collective-permute-start.2 = (f32[1024,256]{1,0:T(8,128)}, f32[1024,256]{1,0:T(8,128)}, u32[]{:S(2)}, u32[]{:S(2)}) collective-permute-start(f32[1024,256]{1,0:T(8,128)} %multiply_add_fusion.1), channel_id=1, source_target_pairs={{0,2},{2,4},{4,6},{6,8},{8,10},{10,12},{12,14},{14,16},{16,18},{18... | collective-permute-start | bytes 3145736 | tf_op jit(solution)/shard_map/ppermute | solution.py:15
  114.9 11.2 %copy-start.2 = (s32[512,1,1024]{0,2,1:T(8,128)S(1)}, s32[512,1,1024]{0,2,1:T(8,128)}, u32[]{:S(2)}) copy-start(s32[512,1,1024]{0,2,1:T(8,128)} %copy.35) | copy-start | bytes 6291460
where the time goes:
time: 140 us; the launch traced here: 139 us
  local copies, waits for them, and re-layouts  47 us (34%)
  matrix products  46.5 us (33%)
  waiting for transfers between devices  32 us (23%)
  starting transfers between devices  11 us (8%)
  other arithmetic  1.85 us (1%)
    unnamed x21, local copies, waits for them, and re-layouts  23.1 us
    slice x1, local copies, waits for them, and re-layouts, body(): values = ratings[:, round_index, :].astype(jnp.float32)  19.8 us
    dot_general x4, matrix products, update(): user_grad = jnp.dot(errors, items, precision=lax.Precision.HIGHEST)  19.8 us
    ppermute x3, waiting for transfers between devices, passed_along(): lax.ppermute(shard, axis, [(i, (i + by) % size) for i in range(size)])  18.8 us
    dot_general x4, matrix products, update(): lax.dot_general(errors, users, (((0,), (0,)), ((), ())), precision=lax.Pr...  13.5 us
    all_to_all x1, waiting for transfers between devices, body(): lax.all_to_all(item_content, 'cat', split_axis=0, concat_axis=1, tiled=True)  13.2 us
    dot_general x4, matrix products, update(): lax.dot_general(users, items, (((1,), (1,)), ((), ())), precision=lax.Pre...  12.8 us
    all_to_all x1, starting transfers between devices, body(): lax.all_to_all(ordered, 'blk', split_axis=0, concat_axis=0, tiled=True)  6.13 us
  transfers between devices with their start and end apart: 5, of which 4 were waited for; matrix products, arithmetic and copies ran while one was open for 42% of the time, Pallas kernels for 0%

commit v1 on v0

v1 whole, which is shorter than its diff:
```python
import functools
import jax
import jax.numpy as jnp
from jax import lax
from jax.experimental import pallas as pl
from jax.experimental.pallas import tpu as pltpu
from jax.sharding import PartitionSpec as P

learn_rate = 0.004
shrink = 0.05
LEVELS = 32000.0
STEPS = 20.0
EXTRA = 16
CHUNK = 256
PARTS = 2


def split(value):
    high = value.astype(jnp.bfloat16)
    return high, (value - high.astype(jnp.float32)).astype(jnp.bfloat16)


def product(left, right, dims):
    def one(a, b):
        return lax.dot_general(a, b, (dims, ((), ())), preferred_element_type=jnp.float32)

    return one(left[0], right[0]) + (one(left[0], right[1]) + one(left[1], right[0]))


def code_of(largest):
    return jnp.ceil(jnp.log(jnp.maximum(largest, 1e-30)) * STEPS)


def step_of(code):
    return jnp.exp(code * (1.0 / STEPS)) * (1.0 / LEVELS)


def coded(value, step):
    return jnp.floor(value * (1.0 / step) + 0.5).astype(jnp.int32).astype(jnp.int16)


def unpack_kernel(in_ref, *out_refs):
    for t, out_ref in enumerate(out_refs):
        out_ref[...] = in_ref[:, t, :].astype(jnp.float32).astype(jnp.bfloat16)


def unpack(ratings):
    users, rounds, items = ratings.shape
    block = min(64, users)
    return pl.pallas_call(
        unpack_kernel,
        grid=(users // block,),
        in_specs=[pl.BlockSpec((block, rounds, items), lambda i: (i, 0, 0))],
        out_specs=[pl.BlockSpec((block, items), lambda i: (i, 0))] * rounds,
        out_shape=[jax.ShapeDtypeStruct((users, items), jnp.bfloat16)] * rounds,
        cost_estimate=pl.CostEstimate(
            flops=1000 * ratings.size, bytes_accessed=6 * ratings.size, transcendentals=0
        ),
        name="unpack",
    )(ratings)


def round_kernel(
    packed_in, packed_out, first, last, users_ref, items_ref, values_ref, grad_ref, users_out, items_out
):
    items, rank = values_ref.shape[1], users_ref.shape[1]
    users = users_ref[...]
    user_parts = split(users)
    chunk = min(CHUNK, items)
    user_grad = jnp.zeros(users.shape, jnp.float32) if first else grad_ref[...]
    if packed_in:
        steps_in = step_of(items_ref[items:, :].astype(jnp.int32).astype(jnp.float32))
    if packed_out:
        row = lax.broadcasted_iota(jnp.int32, (EXTRA, rank), 0)
        codes = jnp.zeros((EXTRA, rank), jnp.float32)
    for n in range(items // chunk):
        at = pl.ds(n * chunk, chunk)
        old = items_ref[at, :]
        if packed_in:
            old = old.astype(jnp.int32).astype(jnp.float32) * steps_in[n : n + 1, :]
        old_parts = split(old)
        guess = product(user_parts, old_parts, ((1,), (1,)))
        values = values_ref[:, at].astype(jnp.float32)
        errors = jnp.where(values > 0.0, values - guess, 0.0)
        error_parts = split(errors)
        item_grad = product(error_parts, user_parts, ((0,), (0,)))
        new = old + learn_rate * (item_grad - shrink * old)
        if packed_out:
            code = code_of(jnp.max(jnp.abs(new), axis=0, keepdims=True))
            codes = jnp.where(row == n, code, codes)
            items_out[at, :] = coded(new, step_of(code))
        else:
            items_out[at, :] = new
        user_grad += product(error_parts, old_parts, ((1,), (0,)))
    if packed_out:
        items_out[pl.ds(items, EXTRA), :] = codes.astype(jnp.int32).astype(jnp.int16)
    if last:
        user_grad = users + learn_rate * (user_grad - shrink * users)
    users_out[...] = user_grad


def update(users, items, values, grad, part, packed_in, packed_out):
    n_users, rank = users.shape
    n_items = values.shape[1] // PARTS
    whole = lambda shape: pl.BlockSpec(shape, lambda i: (0, 0))
    out_items = (
        jax.ShapeDtypeStruct((n_items + EXTRA, rank), jnp.int16)
        if packed_out
        else jax.ShapeDtypeStruct((n_items, rank), jnp.float32)
    )
    return pl.pallas_call(
        functools.partial(round_kernel, packed_in, packed_out, part == 0, part == PARTS - 1),
        grid=(1,),
        in_specs=[
            whole(users.shape),
            whole(items.shape),
            pl.BlockSpec((n_users, n_items), lambda i: (0, part)),
            whole(users.shape),
        ],
        out_specs=[whole(users.shape), whole(out_items.shape)],
        out_shape=[jax.ShapeDtypeStruct(users.shape, jnp.float32), out_items],
        cost_estimate=pl.CostEstimate(
            flops=18 * n_users * n_items * rank, bytes_accessed=5 << 20, transcendentals=0
        ),
        compiler_params=pltpu.CompilerParams(vmem_limit_bytes=48 << 20),
        name="sgd_round",
    )(users, items, values, grad)


def body(item_content, projection, send_order, user_factors, ratings):
    size = lax.axis_size("blk")
    rounds = ratings.shape[1]
    own_rows = lax.all_to_all(item_content, "cat", split_axis=0, concat_axis=1, tiled=True)
    values = unpack(ratings)
    owned = jnp.dot(own_rows, projection, preferred_element_type=jnp.float32)
    ordered = owned.at[send_order[0]].get(mode="promise_in_bounds")
    dealt = ordered.reshape(size, -1, ordered.shape[1])
    share = dealt.shape[1]
    code = code_of(jnp.max(jnp.abs(dealt), axis=1, keepdims=True))
    sent = jnp.concatenate(
        [coded(dealt, step_of(code)), code.astype(jnp.int32).astype(jnp.int16)], axis=1
    )
    got = lax.all_to_all(sent, "blk", split_axis=0, concat_axis=0, tiled=True)
    got = got.astype(jnp.int32).astype(jnp.float32)
    items = (got[:, :share] * step_of(got[:, share:])).reshape(owned.shape)
    users = user_factors
    ring = [(i, (i + 1) % size) for i in range(size)]
    parts = jnp.split(items, PARTS)
    for t in range(rounds):
        grad = users
        sent = []
        for part in range(PARTS):
            grad, moved = update(
                users, parts[part], values[t], grad, part, t > 0, t < rounds - 1
            )
            sent.append(lax.ppermute(moved, "blk", ring) if t < rounds - 1 else moved)
        users, parts = grad, sent
    return (users, jnp.concatenate(parts))


def solution(mesh):
    placed = (
        P("blk", "cat"),
        P(),
        P(("blk", "cat"), None),
        P(("blk", "cat"), None),
        P(("blk", "cat"), None, None),
    )
    return jax.shard_map(
        body,
        mesh=mesh,
        in_specs=placed,
        out_specs=(P(("blk", "cat"), None), P(("blk", "cat"), None)),
        check_vma=False,
    )
```

time: 140 us -> 88.3 us (0.63)
  matrix products: 46.5 us -> 0.47 us
  local copies, waits for them, and re-layouts: 47 us -> 5.37 us
  Pallas kernels: 0 us -> 30.8 us
  waiting for transfers between devices: 32 us -> 36.1 us
    dot_general x12 -> x0, matrix products: 46.1 us -> none  [the longest x4 19.8 us: update(): user_grad = jnp.dot(errors, items, precision=lax.Precision.HIGHEST)]
    pallas_call x0 -> x9, Pallas kernels: none -> 30.8 us  [the longest x8 18 us: update(): pl.pallas_call(functools.partial(round_kernel, packed_in, packed_out, par...]
    unnamed x21 -> x15, local copies, waits for them, and re-layouts: 23.1 us -> 1.27 us
    slice x1 -> x0, local copies, waits for them, and re-layouts: 19.8 us -> none  [body(): values = ratings[:, round_index, :].astype(jnp.float32)]
    all_to_all x1, waiting for transfers between devices: 0.01 us -> 2.63 us  [body(): got = lax.all_to_all(sent, 'blk', split_axis=0, concat_axis=0, tiled=True)]
    concatenate x0 -> x2, other arithmetic: none -> 1.91 us  [the longest x1 1.04 us: body(): return (users, jnp.concatenate(parts))]
    ppermute x3 -> x6, waiting for transfers between devices: 18.8 us -> 19.1 us  [body(): sent.append(lax.ppermute(moved, 'blk', ring) if t < rounds - 1 else moved)]
  transfers between devices with their start and end apart: 5 -> 8, of which waited for: 4 -> 8; matrix products, arithmetic and copies ran while one was open for 42% -> 0% of each run, Pallas kernels for 0% -> 29%
where the time goes in v1:
time: 88.3 us; the launch traced here: 87.9 us
  waiting for transfers between devices  36.1 us (41%)
  Pallas kernels  30.8 us (35%)
  starting transfers between devices  11.8 us (13%)
  local copies, waits for them, and re-layouts  5.37 us (6%)
  other arithmetic  2.53 us (3%)
    ppermute x6, waiting for transfers between devices, body(): sent.append(lax.ppermute(moved, 'blk', ring) if t < rounds - 1 else moved)  19.1 us
    pallas_call x8, Pallas kernels, update(): pl.pallas_call(functools.partial(round_kernel, packed_in, packed_out, par...  18 us
    all_to_all x1, waiting for transfers between devices, body(): lax.all_to_all(item_content, 'cat', split_axis=0, concat_axis=1, tiled=True)  14.4 us
    pallas_call x1, Pallas kernels, unpack(): pl.pallas_call(unpack_kernel, grid=(users // block,), in_specs=[pl.BlockS...  12.7 us
    all_to_all x1, starting transfers between devices, body(): got = lax.all_to_all(sent, 'blk', split_axis=0, concat_axis=0, tiled=True)  6.13 us
    all_to_all x1, starting transfers between devices, body(): lax.all_to_all(item_content, 'cat', split_axis=0, concat_axis=1, tiled=True)  4.41 us
    gather x1, local copies, waits for them, and re-layouts, body(): ordered = owned.at[send_order[0]].get(mode='promise_in_bounds')  3.47 us
    all_to_all x1, waiting for transfers between devices, body(): got = lax.all_to_all(sent, 'blk', split_axis=0, concat_axis=0, tiled=True)  2.63 us
  transfers between devices with their start and end apart: 8, of which 8 were waited for; matrix products, arithmetic and copies ran while one was open for 0% of the time, Pallas kernels for 29%

profile of v1, /device:TPU:0, one launch (start us, length us, event | category | flops | bytes accessed | tf_op | source)
XLA Modules:
  0.0 87.9 jit_solution(4044192784189232028)
XLA Ops:
  0.7 4.4 %all-to-all-start = ((bf16[2,1024,256]{2,1,0:T(8,128)(2,1)}), bf16[2,1024,256]{2,1,0:T(8,128)(2,1)S(1)}, u32[]{:S(2)}, u32[]{:S(2)}) async-start(bf16[2,1024,256]{2,1,0:T(8,128)(2,1)} %bitcast.22), calls=%async_computation | async-start | bytes 2097152 | tf_op jit(solution)/shard_map/all_to_all | solution.py:133
  5.1 14.4 %all-to-all-done = bf16[2,1024,256]{2,1,0:T(8,128)(2,1)S(1)} async-done(((bf16[2,1024,256]{2,1,0:T(8,128)(2,1)}), bf16[2,1024,256]{2,1,0:T(8,128)(2,1)S(1)}, u32[]{:S(2)}, u32[]{:S(2)}) %all-to-all-start) | async-done | bytes 1048608 | tf_op jit(solution)/shard_map/all_to_all | solution.py:133
  19.5 0.5 copy.8
  20.0 0.5 fusion.4
  20.5 3.5 %gather_fusion = f32[1024,256]{1,0:T(8,128)S(1)} fusion(f32[1024,256]{1,0:T(8,128)S(1)} %fusion.4, s32[1024]{0:T(1024)S(1)} %broadcast_clamp_fusion), kind=kCustom, calls=%fused_computation | custom fusion | bytes 2101248 | tf_op jit(solution)/shard_map/gather | solution.py:136
  24.1 0.2 convert_convert_fusion.1
  24.3 0.9 pad_add_fusion
  25.2 6.1 %all-to-all-start.1 = ((s16[16,65,256]{2,1,0:T(8,128)(2,1)}), s16[16,65,256]{2,1,0:T(8,128)(2,1)S(1)}, u32[]{:S(2)}, u32[]{:S(2)}) async-start(s16[16,65,256]{2,1,0:T(8,128)(2,1)} %pad_add_fusion), calls=%async_computation.1 | async-start | bytes 1179648 | tf_op jit(solution)/shard_map/all_to_all | solution.py:143
  31.4 12.7 %unpack.1 = (bf16[512,1024]{1,0:T(8,128)(2,1)}, bf16[512,1024]{1,0:T(8,128)(2,1)}, bf16[512,1024]{1,0:T(8,128)(2,1)}, bf16[512,1024]{1,0:T(8,128)(2,1)}) custom-call(s32[512,4,1024]{2,1,0:T(4,128)} %in_ref.1), custom_call_target="tpu_custom_call" | custom-call | flops 2097152000 | bytes 12582912 | tf_op jit(solution)/shard_map/unpack/pallas_call | solution.py:50
  44.1 2.6 %all-to-all-done.1 = s16[16,65,256]{2,1,0:T(8,128)(2,1)S(1)} async-done(((s16[16,65,256]{2,1,0:T(8,128)(2,1)}), s16[16,65,256]{2,1,0:T(8,128)(2,1)S(1)}, u32[]{:S(2)}, u32[]{:S(2)}) %all-to-all-start.1) | async-done | bytes 532512 | tf_op jit(solution)/shard_map/all_to_all | solution.py:143
  46.7 0.2 convert_convert_fusion
  46.9 0.1 slice_multiply_fusion
  47.2 1.1 %copy-done.4 = bf16[512,1024]{1,0:T(8,128)(2,1)S(1)} copy-done((bf16[512,1024]{1,0:T(8,128)(2,1)S(1)}, bf16[512,1024]{1,0:T(8,128)(2,1)}, u32[]{:S(2)}) %copy-start.4) | copy-done | bytes 1048600
  48.3 0.1 copy-done.5
  48.4 2.1 %sgd_round.8 = (f32[512,256]{1,0:T(8,128)S(1)}, s16[528,256]{1,0:T(8,128)(2,1)S(1)}) custom-call(f32[512,256]{1,0:T(8,128)S(1)} %copy-done.5, f32[512,256]{1,0:T(8,128)S(1)} %bitcast.19, bf16[512,1024]{1,0:T(8,128)(2,1)S(1)} %copy-done.4, f32[512,256]{1,0:T(8,128)S(1)} %copy-done.5), custom_call_target="tpu_custom_call" | custom-call | flops 1207959552 | bytes 5242880 | tf_op jit(solution)/shard_map/sgd_round/pallas_call | solution.py:111
  50.6 0.3 collective-permute-start.1
  50.9 2.2 %sgd_round.9 = (f32[512,256]{1,0:T(8,128)S(1)}, s16[528,256]{1,0:T(8,128)(2,1)S(1)}) custom-call(f32[512,256]{1,0:T(8,128)S(1)} %copy-done.5, f32[512,256]{1,0:T(8,128)S(1)} %bitcast.18, bf16[512,1024]{1,0:T(8,128)(2,1)S(1)} %copy-done.4, f32[512,256]{1,0:T(8,128)S(1)} %get-tuple-element.23.grad_ref), custom_call_target="tpu_custom_call" | custom-call | flops 1207959552 | bytes 5242880 | tf_op jit(solution)/shard_map/sgd_round/pallas_call | solution.py:111
  53.0 0.6 collective-permute-start
  53.6 5.6 %collective-permute-done.1.items_ref = s16[528,256]{1,0:T(8,128)(2,1)S(1)} collective-permute-done((s16[528,256]{1,0:T(8,128)(2,1)S(1)}, s16[528,256]{1,0:T(8,128)(2,1)S(1)}, u32[]{:S(2)}, u32[]{:S(2)}) %collective-permute-start.1) | collective-permute-done | bytes 270368 | tf_op jit(solution)/shard_map/ppermute | solution.py:156
  59.2 2.2 %sgd_round.10 = (f32[512,256]{1,0:T(8,128)S(1)}, s16[528,256]{1,0:T(8,128)(2,1)S(1)}) custom-call(f32[512,256]{1,0:T(8,128)S(1)} %get-tuple-element.24.users_ref.grad_ref, s16[528,256]{1,0:T(8,128)(2,1)S(1)} %collective-permute-done.1.items_ref, bf16[512,1024]{1,0:T(8,128)(2,1)S(1)} %copy-done.3, f32[512,256]{1,0:T(8,128)S(1)} %get-tuple-element.24.users_ref.grad_ref), custom_call_target="tpu_custom_call" | custom-call | flops 1207959552 | bytes 5242880 | tf_op jit(solution)/shard_map/sgd_round/pallas_call | solution.py:111
  61.4 0.7 collective-permute-done.items_ref
  62.1 2.2 %sgd_round.11 = (f32[512,256]{1,0:T(8,128)S(1)}, s16[528,256]{1,0:T(8,128)(2,1)S(1)}) custom-call(f32[512,256]{1,0:T(8,128)S(1)} %get-tuple-element.24.users_ref.grad_ref, s16[528,256]{1,0:T(8,128)(2,1)S(1)} %collective-permute-done.items_ref, bf16[512,1024]{1,0:T(8,128)(2,1)S(1)} %copy-done.3, f32[512,256]{1,0:T(8,128)S(1)} %get-tuple-element.28.grad_ref), custom_call_target="tpu_custom_call" | custom-call | flops 1207959552 | bytes 5242880 | tf_op jit(solution)/shard_map/sgd_round/pallas_call | solution.py:111
  64.3 0.2 collective-permute-start.2
  64.5 5.5 %collective-permute-done.3.items_ref = s16[528,256]{1,0:T(8,128)(2,1)S(1)} collective-permute-done((s16[528,256]{1,0:T(8,128)(2,1)S(1)}, s16[528,256]{1,0:T(8,128)(2,1)S(1)}, u32[]{:S(2)}, u32[]{:S(2)}) %collective-permute-start.3) | collective-permute-done | bytes 270368 | tf_op jit(solution)/shard_map/ppermute | solution.py:156
  70.0 2.2 %sgd_round.12 = (f32[512,256]{1,0:T(8,128)S(1)}, s16[528,256]{1,0:T(8,128)(2,1)S(1)}) custom-call(f32[512,256]{1,0:T(8,128)S(1)} %get-tuple-element.29.users_ref.grad_ref, s16[528,256]{1,0:T(8,128)(2,1)S(1)} %collective-permute-done.3.items_ref, bf16[512,1024]{1,0:T(8,128)(2,1)S(1)} %copy-done.2, f32[512,256]{1,0:T(8,128)S(1)} %get-tuple-element.29.users_ref.grad_ref), custom_call_target="tpu_custom_call" | custom-call | flops 1207959552 | bytes 5242880 | tf_op jit(solution)/shard_map/sgd_round/pallas_call | solution.py:111
  72.3 0.8 collective-permute-done.2.items_ref
  73.1 2.2 %sgd_round.13 = (f32[512,256]{1,0:T(8,128)S(1)}, s16[528,256]{1,0:T(8,128)(2,1)S(1)}) custom-call(f32[512,256]{1,0:T(8,128)S(1)} %get-tuple-element.29.users_ref.grad_ref, s16[528,256]{1,0:T(8,128)(2,1)S(1)} %collective-permute-done.2.items_ref, bf16[512,1024]{1,0:T(8,128)(2,1)S(1)} %copy-done.2, f32[512,256]{1,0:T(8,128)S(1)} %get-tuple-element.33.grad_ref), custom_call_target="tpu_custom_call" | custom-call | flops 1207959552 | bytes 5242880 | tf_op jit(solution)/shard_map/sgd_round/pallas_call | solution.py:111
  75.4 5.5 %collective-permute-done.5.items_ref = s16[528,256]{1,0:T(8,128)(2,1)S(1)} collective-permute-done((s16[528,256]{1,0:T(8,128)(2,1)S(1)}, s16[528,256]{1,0:T(8,128)(2,1)S(1)}, u32[]{:S(2)}, u32[]{:S(2)}) %collective-permute-start.5) | collective-permute-done | bytes 270368 | tf_op jit(solution)/shard_map/ppermute | solution.py:156
  80.8 2.1 %sgd_round.14 = (f32[512,256]{1,0:T(8,128)S(1)}, f32[512,256]{1,0:T(8,128)S(1)}) custom-call(f32[512,256]{1,0:T(8,128)S(1)} %get-tuple-element.34.users_ref.grad_ref, s16[528,256]{1,0:T(8,128)(2,1)S(1)} %collective-permute-done.5.items_ref, bf16[512,1024]{1,0:T(8,128)(2,1)S(1)} %copy-done.1, f32[512,256]{1,0:T(8,128)S(1)} %get-tuple-element.34.users_ref.grad_ref), custom_call_target="tpu_custom_call" | custom-call | flops 1207959552 | bytes 5242880 | tf_op jit(solution)/shard_map/sgd_round/pallas_call | solution.py:111
  83.0 1.0 %collective-permute-done.4.items_ref = s16[528,256]{1,0:T(8,128)(2,1)S(1)} collective-permute-done((s16[528,256]{1,0:T(8,128)(2,1)S(1)}, s16[528,256]{1,0:T(8,128)(2,1)S(1)}, u32[]{:S(2)}, u32[]{:S(2)}) %collective-permute-start.4) | collective-permute-done | bytes 270368 | tf_op jit(solution)/shard_map/ppermute | solution.py:156
  83.9 2.9 %sgd_round.15 = (f32[512,256]{1,0:T(8,128)}, f32[512,256]{1,0:T(8,128)S(1)}) custom-call(f32[512,256]{1,0:T(8,128)S(1)} %get-tuple-element.34.users_ref.grad_ref, s16[528,256]{1,0:T(8,128)(2,1)S(1)} %collective-permute-done.4.items_ref, bf16[512,1024]{1,0:T(8,128)(2,1)S(1)} %copy-done.1, f32[512,256]{1,0:T(8,128)S(1)} %get-tuple-element.38.grad_ref), custom_call_target="tpu_custom_call" | custom-call | flops 1207959552 | bytes 5242880 | tf_op jit(solution)/shard_map/sgd_round/pallas_call | solution.py:111
  86.8 1.0 %pad_maximum_fusion = f32[1024,256]{1,0:T(8,128)} fusion(f32[512,256]{1,0:T(8,128)S(1)} %get-tuple-element.41, f32[512,256]{1,0:T(8,128)S(1)} %get-tuple-element.40), kind=kLoop, calls=%fused_computation.3 | loop fusion | flops 262144 | bytes 2097152 | tf_op jit(solution)/shard_map/concatenate | solution.py:158
  (23 shorter events, 0.5 us)
Async XLA Ops:
  0.6 19.4 %copy-start = (bf16[512,256]{1,0:T(8,128)(2,1)S(1)}, bf16[512,256]{1,0:T(8,128)(2,1)}, u32[]{:S(2)}) copy-start(bf16[512,256]{1,0:T(8,128)(2,1)} %param.6) | copy-start | bytes 786436
  0.6 4.4 %copy-start.6 = (s32[1,1024]{1,0:T(1,128)S(1)}, s32[1,1024]{1,0:T(1,128)}, u32[]{:S(2)}) copy-start(s32[1,1024]{1,0:T(1,128)} %param.7) | copy-start | bytes 12292
  0.7 18.8 %all-to-all-start = ((bf16[2,1024,256]{2,1,0:T(8,128)(2,1)}), bf16[2,1024,256]{2,1,0:T(8,128)(2,1)S(1)}, u32[]{:S(2)}, u32[]{:S(2)}) async-start(bf16[2,1024,256]{2,1,0:T(8,128)(2,1)} %bitcast.22), calls=%async_computation | async-start | bytes 2097152 | tf_op jit(solution)/shard_map/all_to_all | solution.py:133
  25.2 21.5 %all-to-all-start.1 = ((s16[16,65,256]{2,1,0:T(8,128)(2,1)}), s16[16,65,256]{2,1,0:T(8,128)(2,1)S(1)}, u32[]{:S(2)}, u32[]{:S(2)}) async-start(s16[16,65,256]{2,1,0:T(8,128)(2,1)} %pad_add_fusion), calls=%async_computation.1 | async-start | bytes 1179648 | tf_op jit(solution)/shard_map/all_to_all | solution.py:143
  47.1 1.2 %copy-start.4 = (bf16[512,1024]{1,0:T(8,128)(2,1)S(1)}, bf16[512,1024]{1,0:T(8,128)(2,1)}, u32[]{:S(2)}) copy-start(bf16[512,1024]{1,0:T(8,128)(2,1)} %get-tuple-element.22.values_ref) | copy-start | bytes 3145732
  47.1 1.3 %copy-start.5 = (f32[512,256]{1,0:T(8,128)S(1)}, f32[512,256]{1,0:T(8,128)}, u32[]{:S(2)}) copy-start(f32[512,256]{1,0:T(8,128)} %users_ref.3) | copy-start | bytes 1572868
  50.6 8.6 %collective-permute-start.1 = (s16[528,256]{1,0:T(8,128)(2,1)S(1)}, s16[528,256]{1,0:T(8,128)(2,1)S(1)}, u32[]{:S(2)}, u32[]{:S(2)}) collective-permute-start(s16[528,256]{1,0:T(8,128)(2,1)S(1)} %get-tuple-element.27), channel_id=1, source_target_pairs={{0,2},{2,4},{4,6},{6,8},{8,10},{10,12},{12,14},{14,16},{16,18},{18... | collective-permute-start | bytes 811016 | tf_op jit(solution)/shard_map/ppermute | solution.py:156
  50.9 8.4 %copy-start.3 = (bf16[512,1024]{1,0:T(8,128)(2,1)S(1)}, bf16[512,1024]{1,0:T(8,128)(2,1)}, u32[]{:S(2)}) copy-start(bf16[512,1024]{1,0:T(8,128)(2,1)} %get-tuple-element.26.values_ref) | copy-start | bytes 3145732
  53.0 9.1 %collective-permute-start = (s16[528,256]{1,0:T(8,128)(2,1)S(1)}, s16[528,256]{1,0:T(8,128)(2,1)S(1)}, u32[]{:S(2)}, u32[]{:S(2)}) collective-permute-start(s16[528,256]{1,0:T(8,128)(2,1)S(1)} %get-tuple-element.25), channel_id=1, source_target_pairs={{0,2},{2,4},{4,6},{6,8},{8,10},{10,12},{12,14},{14,16},{16,18},{18... | collective-permute-start | bytes 811016 | tf_op jit(solution)/shard_map/ppermute | solution.py:156
  61.4 8.6 %collective-permute-start.3 = (s16[528,256]{1,0:T(8,128)(2,1)S(1)}, s16[528,256]{1,0:T(8,128)(2,1)S(1)}, u32[]{:S(2)}, u32[]{:S(2)}) collective-permute-start(s16[528,256]{1,0:T(8,128)(2,1)S(1)} %get-tuple-element.32), channel_id=1, source_target_pairs={{0,2},{2,4},{4,6},{6,8},{8,10},{10,12},{12,14},{14,16},{16,18},{18... | collective-permute-start | bytes 811016 | tf_op jit(solution)/shard_map/ppermute | solution.py:156
  62.1 7.9 %copy-start.2 = (bf16[512,1024]{1,0:T(8,128)(2,1)S(1)}, bf16[512,1024]{1,0:T(8,128)(2,1)}, u32[]{:S(2)}) copy-start(bf16[512,1024]{1,0:T(8,128)(2,1)} %get-tuple-element.31.values_ref) | copy-start | bytes 3145732
  64.3 8.8 %collective-permute-start.2 = (s16[528,256]{1,0:T(8,128)(2,1)S(1)}, s16[528,256]{1,0:T(8,128)(2,1)S(1)}, u32[]{:S(2)}, u32[]{:S(2)}) collective-permute-start(s16[528,256]{1,0:T(8,128)(2,1)S(1)} %get-tuple-element.30), channel_id=1, source_target_pairs={{0,2},{2,4},{4,6},{6,8},{8,10},{10,12},{12,14},{14,16},{16,18},{18... | collective-permute-start | bytes 811016 | tf_op jit(solution)/shard_map/ppermute | solution.py:156
  72.2 8.6 %collective-permute-start.5 = (s16[528,256]{1,0:T(8,128)(2,1)S(1)}, s16[528,256]{1,0:T(8,128)(2,1)S(1)}, u32[]{:S(2)}, u32[]{:S(2)}) collective-permute-start(s16[528,256]{1,0:T(8,128)(2,1)S(1)} %get-tuple-element.37), channel_id=1, source_target_pairs={{0,2},{2,4},{4,6},{6,8},{8,10},{10,12},{12,14},{14,16},{16,18},{18... | collective-permute-start | bytes 811016 | tf_op jit(solution)/shard_map/ppermute | solution.py:156
  73.1 7.7 %copy-start.1 = (bf16[512,1024]{1,0:T(8,128)(2,1)S(1)}, bf16[512,1024]{1,0:T(8,128)(2,1)}, u32[]{:S(2)}) copy-start(bf16[512,1024]{1,0:T(8,128)(2,1)} %get-tuple-element.36.values_ref) | copy-start | bytes 3145732
  75.3 8.6 %collective-permute-start.4 = (s16[528,256]{1,0:T(8,128)(2,1)S(1)}, s16[528,256]{1,0:T(8,128)(2,1)S(1)}, u32[]{:S(2)}, u32[]{:S(2)}) collective-permute-start(s16[528,256]{1,0:T(8,128)(2,1)S(1)} %get-tuple-element.35), channel_id=1, source_target_pairs={{0,2},{2,4},{4,6},{6,8},{8,10},{10,12},{12,14},{14,16},{16,18},{18... | collective-permute-start | bytes 811016 | tf_op jit(solution)/shard_map/ppermute | solution.py:156

commit v2 on v1

--- a/solution.py
+++ b/solution.py
@@ -127,12 +127,28 @@
     )(users, items, values, grad)
 
 
+def project(item_content, projection):
+    def dot(rows, weights):
+        return jnp.dot(rows, weights, preferred_element_type=jnp.float32)
+
+    if lax.axis_size("cat") != 2:
+        rows = lax.all_to_all(item_content, "cat", split_axis=0, concat_axis=1, tiled=True)
+        return dot(rows, projection)
+    me = lax.axis_index("cat")
+    rows, width = item_content.shape[0] // 2, item_content.shape[1]
+    other = 1 - me
+    theirs = lax.dynamic_slice_in_dim(item_content, other * rows, rows)
+    got = lax.ppermute(theirs, "cat", [(0, 1), (1, 0)])
+    mine = lax.dynamic_slice_in_dim(item_content, me * rows, rows)
+    near = dot(mine, lax.dynamic_slice_in_dim(projection, me * width, width))
+    return near + dot(got, lax.dynamic_slice_in_dim(projection, other * width, width))
+
+
 def body(item_content, projection, send_order, user_factors, ratings):
     size = lax.axis_size("blk")
     rounds = ratings.shape[1]
-    own_rows = lax.all_to_all(item_content, "cat", split_axis=0, concat_axis=1, tiled=True)
     values = unpack(ratings)
-    owned = jnp.dot(own_rows, projection, preferred_element_type=jnp.float32)
+    owned = project(item_content, projection)
     ordered = owned.at[send_order[0]].get(mode="promise_in_bounds")
     dealt = ordered.reshape(size, -1, ordered.shape[1])
     share = dealt.shape[1]

time: 88.3 us -> 84.9 us (0.961)
  waiting for transfers between devices: 36.1 us -> 32.3 us
  starting transfers between devices: 11.8 us -> 10.4 us
  matrix products: 0.47 us -> 1.5 us
    all_to_all x1 -> x0, waiting for transfers between devices: 14.4 us -> none  [body(): lax.all_to_all(item_content, 'cat', split_axis=0, concat_axis=1, tiled=True)]
    ppermute x0 -> x1, waiting for transfers between devices: none -> 10.7 us  [project(): got = lax.ppermute(theirs, 'cat', [(0, 1), (1, 0)])]
    all_to_all x1 -> x0, starting transfers between devices: 4.41 us -> none  [body(): lax.all_to_all(item_content, 'cat', split_axis=0, concat_axis=1, tiled=True)]
    ppermute x0 -> x1, starting transfers between devices: none -> 3.06 us  [project(): got = lax.ppermute(theirs, 'cat', [(0, 1), (1, 0)])]
    unnamed x15 -> x17, local copies, waits for them, and re-layouts: 1.27 us -> 2.48 us
    dot_general x1 -> x2, matrix products: 0.47 us -> 1.5 us  [dot(): return jnp.dot(rows, weights, preferred_element_type=jnp.float32)]
  transfers between devices with their start and end apart: 8 -> 8, of which waited for: 8 -> 8; matrix products, arithmetic and copies ran while one was open for 0% -> 1% of each run, Pallas kernels for 29% -> 30%
where the time goes in v2:
time: 84.9 us; the launch traced here: 84.6 us
  waiting for transfers between devices  32.3 us (38%)
  Pallas kernels  30.8 us (36%)
  starting transfers between devices  10.4 us (12%)
  local copies, waits for them, and re-layouts  6.09 us (7%)
  other arithmetic  2.53 us (3%)
  matrix products  1.5 us (2%)
  between operations  0.87 us (1%)
    ppermute x6, waiting for transfers between devices, body(): sent.append(lax.ppermute(moved, 'blk', ring) if t < rounds - 1 else moved)  19 us
    pallas_call x8, Pallas kernels, update(): pl.pallas_call(functools.partial(round_kernel, packed_in, packed_out, par...  18.1 us
    pallas_call x1, Pallas kernels, unpack(): pl.pallas_call(unpack_kernel, grid=(users // block,), in_specs=[pl.BlockS...  12.7 us
    ppermute x1, waiting for transfers between devices, project(): got = lax.ppermute(theirs, 'cat', [(0, 1), (1, 0)])  10.7 us
    all_to_all x1, starting transfers between devices, body(): got = lax.all_to_all(sent, 'blk', split_axis=0, concat_axis=0, tiled=True)  6.13 us
    gather x1, local copies, waits for them, and re-layouts, body(): ordered = owned.at[send_order[0]].get(mode='promise_in_bounds')  3.47 us
    ppermute x1, starting transfers between devices, project(): got = lax.ppermute(theirs, 'cat', [(0, 1), (1, 0)])  3.06 us
    all_to_all x1, waiting for transfers between devices, body(): got = lax.all_to_all(sent, 'blk', split_axis=0, concat_axis=0, tiled=True)  2.63 us
  transfers between devices with their start and end apart: 8, of which 8 were waited for; matrix products, arithmetic and copies ran while one was open for 1% of the time, Pallas kernels for 30%

profile of v2, /device:TPU:0, one launch (start us, length us, event | category | flops | bytes accessed | tf_op | source)
XLA Modules:
  0.0 84.6 jit_solution(5607522023987395920)
XLA Ops:
  0.6 1.2 %copy-done = bf16[2048,256]{1,0:T(8,128)(2,1)S(1)} copy-done((bf16[2048,256]{1,0:T(8,128)(2,1)S(1)}, bf16[2048,256]{1,0:T(8,128)(2,1)}, u32[]{:S(2)}) %copy-start) | copy-done | bytes 1048600
  1.9 3.1 %collective-permute-start = (bf16[1024,256]{1,0:T(8,128)(2,1)S(1)}, bf16[1024,256]{1,0:T(8,128)(2,1)S(1)}, u32[]{:S(2)}, u32[]{:S(2)}) collective-permute-start(bf16[1024,256]{1,0:T(8,128)(2,1)S(1)} %constant_dynamic-slice_fusion), channel_id=1, source_target_pairs={{0,1},{1,0},{2,3},{3,2},{4,5},{5,4},{6,7},{7,6},{8,9},{9,8},{10,11... | collective-permute-start | bytes 1572872 | tf_op jit(solution)/shard_map/ppermute | solution.py:141
  5.0 1.2 %fusion = f32[1024,256]{1,0:T(8,128)S(1)} fusion(bf16[2048,256]{1,0:T(8,128)(2,1)S(1)} %copy-done, s32[]{:T(128)S(6)} %select_n.22, bf16[512,256]{1,0:T(8,128)(2,1)} %param.6, s32[]{:T(128)S(6)} %select_n.23), kind=kOutput, calls=%fused_computation.8 | convolution fusion | flops 134217728 | bytes 1703944 | tf_op jit(solution)/shard_map/dot_general | solution.py:132
  6.2 10.7 %collective-permute-done = bf16[1024,256]{1,0:T(8,128)(2,1)S(1)} collective-permute-done((bf16[1024,256]{1,0:T(8,128)(2,1)S(1)}, bf16[1024,256]{1,0:T(8,128)(2,1)S(1)}, u32[]{:S(2)}, u32[]{:S(2)}) %collective-permute-start) | collective-permute-done | bytes 524320 | tf_op jit(solution)/shard_map/ppermute | solution.py:141
  16.9 0.3 convolution_add_fusion
  17.2 3.5 %gather_fusion = f32[1024,256]{1,0:T(8,128)S(1)} fusion(f32[1024,256]{1,0:T(8,128)S(1)} %convolution_add_fusion, s32[1024]{0:T(1024)S(1)} %broadcast_clamp_fusion), kind=kCustom, calls=%fused_computation | custom fusion | bytes 2101248 | tf_op jit(solution)/shard_map/gather | solution.py:152
  20.8 0.2 convert_convert_fusion.1
  21.0 0.9 %pad_add_fusion = s16[16,65,256]{2,1,0:T(8,128)(2,1)} fusion(s16[16,1,256]{2,1,0:T(2,128)(2,1)S(1)} %copy.7, s16[16,64,256]{2,1,0:T(8,128)(2,1)S(1)} %convert_convert_fusion.1), kind=kLoop, calls=%fused_computation.7 | loop fusion | flops 266240 | bytes 1064960 | tf_op jit(solution)/shard_map/concatenate | solution.py:156
  21.9 6.1 %all-to-all-start = ((s16[16,65,256]{2,1,0:T(8,128)(2,1)}), s16[16,65,256]{2,1,0:T(8,128)(2,1)S(1)}, u32[]{:S(2)}, u32[]{:S(2)}) async-start(s16[16,65,256]{2,1,0:T(8,128)(2,1)} %pad_add_fusion), calls=%async_computation | async-start | bytes 1179648 | tf_op jit(solution)/shard_map/all_to_all | solution.py:159
  28.0 12.7 %unpack.1 = (bf16[512,1024]{1,0:T(8,128)(2,1)}, bf16[512,1024]{1,0:T(8,128)(2,1)}, bf16[512,1024]{1,0:T(8,128)(2,1)}, bf16[512,1024]{1,0:T(8,128)(2,1)}) custom-call(s32[512,4,1024]{2,1,0:T(4,128)} %in_ref.1), custom_call_target="tpu_custom_call" | custom-call | flops 2097152000 | bytes 12582912 | tf_op jit(solution)/shard_map/unpack/pallas_call | solution.py:50
  40.8 2.6 %all-to-all-done = s16[16,65,256]{2,1,0:T(8,128)(2,1)S(1)} async-done(((s16[16,65,256]{2,1,0:T(8,128)(2,1)}), s16[16,65,256]{2,1,0:T(8,128)(2,1)S(1)}, u32[]{:S(2)}, u32[]{:S(2)}) %all-to-all-start) | async-done | bytes 532512 | tf_op jit(solution)/shard_map/all_to_all | solution.py:159
  43.4 0.2 convert_convert_fusion
  43.9 1.1 %copy-done.4 = bf16[512,1024]{1,0:T(8,128)(2,1)S(1)} copy-done((bf16[512,1024]{1,0:T(8,128)(2,1)S(1)}, bf16[512,1024]{1,0:T(8,128)(2,1)}, u32[]{:S(2)}) %copy-start.4) | copy-done | bytes 1048600
  45.0 0.1 copy-done.5
  45.1 2.2 %sgd_round.8 = (f32[512,256]{1,0:T(8,128)S(1)}, s16[528,256]{1,0:T(8,128)(2,1)S(1)}) custom-call(f32[512,256]{1,0:T(8,128)S(1)} %copy-done.5, f32[512,256]{1,0:T(8,128)S(1)} %bitcast.15, bf16[512,1024]{1,0:T(8,128)(2,1)S(1)} %copy-done.4, f32[512,256]{1,0:T(8,128)S(1)} %copy-done.5), custom_call_target="tpu_custom_call" | custom-call | flops 1207959552 | bytes 5242880 | tf_op jit(solution)/shard_map/sgd_round/pallas_call | solution.py:111
  47.3 0.3 collective-permute-start.2
  47.5 2.2 %sgd_round.9 = (f32[512,256]{1,0:T(8,128)S(1)}, s16[528,256]{1,0:T(8,128)(2,1)S(1)}) custom-call(f32[512,256]{1,0:T(8,128)S(1)} %copy-done.5, f32[512,256]{1,0:T(8,128)S(1)} %bitcast.14, bf16[512,1024]{1,0:T(8,128)(2,1)S(1)} %copy-done.4, f32[512,256]{1,0:T(8,128)S(1)} %get-tuple-element.23.grad_ref), custom_call_target="tpu_custom_call" | custom-call | flops 1207959552 | bytes 5242880 | tf_op jit(solution)/shard_map/sgd_round/pallas_call | solution.py:111
  49.7 0.6 collective-permute-start.1
  50.3 5.6 %collective-permute-done.2.items_ref = s16[528,256]{1,0:T(8,128)(2,1)S(1)} collective-permute-done((s16[528,256]{1,0:T(8,128)(2,1)S(1)}, s16[528,256]{1,0:T(8,128)(2,1)S(1)}, u32[]{:S(2)}, u32[]{:S(2)}) %collective-permute-start.2) | collective-permute-done | bytes 270368 | tf_op jit(solution)/shard_map/ppermute | solution.py:172
  55.9 2.2 %sgd_round.10 = (f32[512,256]{1,0:T(8,128)S(1)}, s16[528,256]{1,0:T(8,128)(2,1)S(1)}) custom-call(f32[512,256]{1,0:T(8,128)S(1)} %get-tuple-element.24.users_ref.grad_ref, s16[528,256]{1,0:T(8,128)(2,1)S(1)} %collective-permute-done.2.items_ref, bf16[512,1024]{1,0:T(8,128)(2,1)S(1)} %copy-done.3, f32[512,256]{1,0:T(8,128)S(1)} %get-tuple-element.24.users_ref.grad_ref), custom_call_target="tpu_custom_call" | custom-call | flops 1207959552 | bytes 5242880 | tf_op jit(solution)/shard_map/sgd_round/pallas_call | solution.py:111
  58.1 0.7 collective-permute-done.1.items_ref
  58.8 2.2 %sgd_round.11 = (f32[512,256]{1,0:T(8,128)S(1)}, s16[528,256]{1,0:T(8,128)(2,1)S(1)}) custom-call(f32[512,256]{1,0:T(8,128)S(1)} %get-tuple-element.24.users_ref.grad_ref, s16[528,256]{1,0:T(8,128)(2,1)S(1)} %collective-permute-done.1.items_ref, bf16[512,1024]{1,0:T(8,128)(2,1)S(1)} %copy-done.3, f32[512,256]{1,0:T(8,128)S(1)} %get-tuple-element.28.grad_ref), custom_call_target="tpu_custom_call" | custom-call | flops 1207959552 | bytes 5242880 | tf_op jit(solution)/shard_map/sgd_round/pallas_call | solution.py:111
  61.0 0.2 collective-permute-start.3
  61.2 5.5 %collective-permute-done.4.items_ref = s16[528,256]{1,0:T(8,128)(2,1)S(1)} collective-permute-done((s16[528,256]{1,0:T(8,128)(2,1)S(1)}, s16[528,256]{1,0:T(8,128)(2,1)S(1)}, u32[]{:S(2)}, u32[]{:S(2)}) %collective-permute-start.4) | collective-permute-done | bytes 270368 | tf_op jit(solution)/shard_map/ppermute | solution.py:172
  66.7 2.2 %sgd_round.12 = (f32[512,256]{1,0:T(8,128)S(1)}, s16[528,256]{1,0:T(8,128)(2,1)S(1)}) custom-call(f32[512,256]{1,0:T(8,128)S(1)} %get-tuple-element.29.users_ref.grad_ref, s16[528,256]{1,0:T(8,128)(2,1)S(1)} %collective-permute-done.4.items_ref, bf16[512,1024]{1,0:T(8,128)(2,1)S(1)} %copy-done.2, f32[512,256]{1,0:T(8,128)S(1)} %get-tuple-element.29.users_ref.grad_ref), custom_call_target="tpu_custom_call" | custom-call | flops 1207959552 | bytes 5242880 | tf_op jit(solution)/shard_map/sgd_round/pallas_call | solution.py:111
  68.9 0.8 collective-permute-done.3.items_ref
  69.8 2.2 %sgd_round.13 = (f32[512,256]{1,0:T(8,128)S(1)}, s16[528,256]{1,0:T(8,128)(2,1)S(1)}) custom-call(f32[512,256]{1,0:T(8,128)S(1)} %get-tuple-element.29.users_ref.grad_ref, s16[528,256]{1,0:T(8,128)(2,1)S(1)} %collective-permute-done.3.items_ref, bf16[512,1024]{1,0:T(8,128)(2,1)S(1)} %copy-done.2, f32[512,256]{1,0:T(8,128)S(1)} %get-tuple-element.33.grad_ref), custom_call_target="tpu_custom_call" | custom-call | flops 1207959552 | bytes 5242880 | tf_op jit(solution)/shard_map/sgd_round/pallas_call | solution.py:111
  72.0 5.5 %collective-permute-done.6.items_ref = s16[528,256]{1,0:T(8,128)(2,1)S(1)} collective-permute-done((s16[528,256]{1,0:T(8,128)(2,1)S(1)}, s16[528,256]{1,0:T(8,128)(2,1)S(1)}, u32[]{:S(2)}, u32[]{:S(2)}) %collective-permute-start.6) | collective-permute-done | bytes 270368 | tf_op jit(solution)/shard_map/ppermute | solution.py:172
  77.5 2.1 %sgd_round.14 = (f32[512,256]{1,0:T(8,128)S(1)}, f32[512,256]{1,0:T(8,128)S(1)}) custom-call(f32[512,256]{1,0:T(8,128)S(1)} %get-tuple-element.34.users_ref.grad_ref, s16[528,256]{1,0:T(8,128)(2,1)S(1)} %collective-permute-done.6.items_ref, bf16[512,1024]{1,0:T(8,128)(2,1)S(1)} %copy-done.1, f32[512,256]{1,0:T(8,128)S(1)} %get-tuple-element.34.users_ref.grad_ref), custom_call_target="tpu_custom_call" | custom-call | flops 1207959552 | bytes 5242880 | tf_op jit(solution)/shard_map/sgd_round/pallas_call | solution.py:111
  79.6 1.0 %collective-permute-done.5.items_ref = s16[528,256]{1,0:T(8,128)(2,1)S(1)} collective-permute-done((s16[528,256]{1,0:T(8,128)(2,1)S(1)}, s16[528,256]{1,0:T(8,128)(2,1)S(1)}, u32[]{:S(2)}, u32[]{:S(2)}) %collective-permute-start.5) | collective-permute-done | bytes 270368 | tf_op jit(solution)/shard_map/ppermute | solution.py:172
  80.6 2.9 %sgd_round.15 = (f32[512,256]{1,0:T(8,128)}, f32[512,256]{1,0:T(8,128)S(1)}) custom-call(f32[512,256]{1,0:T(8,128)S(1)} %get-tuple-element.34.users_ref.grad_ref, s16[528,256]{1,0:T(8,128)(2,1)S(1)} %collective-permute-done.5.items_ref, bf16[512,1024]{1,0:T(8,128)(2,1)S(1)} %copy-done.1, f32[512,256]{1,0:T(8,128)S(1)} %get-tuple-element.38.grad_ref), custom_call_target="tpu_custom_call" | custom-call | flops 1207959552 | bytes 5242880 | tf_op jit(solution)/shard_map/sgd_round/pallas_call | solution.py:111
  83.5 1.0 %pad_maximum_fusion = f32[1024,256]{1,0:T(8,128)} fusion(f32[512,256]{1,0:T(8,128)S(1)} %get-tuple-element.41, f32[512,256]{1,0:T(8,128)S(1)} %get-tuple-element.40), kind=kLoop, calls=%fused_computation.4 | loop fusion | flops 262144 | bytes 2097152 | tf_op jit(solution)/shard_map/concatenate | solution.py:174
  (26 shorter events, 0.6 us)
Async XLA Ops:
  0.6 1.2 %copy-start = (bf16[2048,256]{1,0:T(8,128)(2,1)S(1)}, bf16[2048,256]{1,0:T(8,128)(2,1)}, u32[]{:S(2)}) copy-start(bf16[2048,256]{1,0:T(8,128)(2,1)} %param.5) | copy-start | bytes 3145732
  1.9 4.3 %copy-start.7 = (s32[1,1024]{1,0:T(1,128)S(1)}, s32[1,1024]{1,0:T(1,128)}, u32[]{:S(2)}) copy-start(s32[1,1024]{1,0:T(1,128)} %param.7) | copy-start | bytes 12292
  1.9 15.0 %copy-start.6 = (bf16[512,256]{1,0:T(8,128)(2,1)S(1)}, bf16[512,256]{1,0:T(8,128)(2,1)}, u32[]{:S(2)}) copy-start(bf16[512,256]{1,0:T(8,128)(2,1)} %param.6) | copy-start | bytes 786436
  1.9 15.0 %collective-permute-start = (bf16[1024,256]{1,0:T(8,128)(2,1)S(1)}, bf16[1024,256]{1,0:T(8,128)(2,1)S(1)}, u32[]{:S(2)}, u32[]{:S(2)}) collective-permute-start(bf16[1024,256]{1,0:T(8,128)(2,1)S(1)} %constant_dynamic-slice_fusion), channel_id=1, source_target_pairs={{0,1},{1,0},{2,3},{3,2},{4,5},{5,4},{6,7},{7,6},{8,9},{9,8},{10,11... | collective-permute-start | bytes 1572872 | tf_op jit(solution)/shard_map/ppermute | solution.py:141
  21.9 21.5 %all-to-all-start = ((s16[16,65,256]{2,1,0:T(8,128)(2,1)}), s16[16,65,256]{2,1,0:T(8,128)(2,1)S(1)}, u32[]{:S(2)}, u32[]{:S(2)}) async-start(s16[16,65,256]{2,1,0:T(8,128)(2,1)} %pad_add_fusion), calls=%async_computation | async-start | bytes 1179648 | tf_op jit(solution)/shard_map/all_to_all | solution.py:159
  43.7 1.2 %copy-start.4 = (bf16[512,1024]{1,0:T(8,128)(2,1)S(1)}, bf16[512,1024]{1,0:T(8,128)(2,1)}, u32[]{:S(2)}) copy-start(bf16[512,1024]{1,0:T(8,128)(2,1)} %get-tuple-element.22.values_ref) | copy-start | bytes 3145732
  43.7 1.3 %copy-start.5 = (f32[512,256]{1,0:T(8,128)S(1)}, f32[512,256]{1,0:T(8,128)}, u32[]{:S(2)}) copy-start(f32[512,256]{1,0:T(8,128)} %users_ref.3) | copy-start | bytes 1572868
  47.3 8.6 %collective-permute-start.2 = (s16[528,256]{1,0:T(8,128)(2,1)S(1)}, s16[528,256]{1,0:T(8,128)(2,1)S(1)}, u32[]{:S(2)}, u32[]{:S(2)}) collective-permute-start(s16[528,256]{1,0:T(8,128)(2,1)S(1)} %get-tuple-element.27), channel_id=1, source_target_pairs={{0,2},{2,4},{4,6},{6,8},{8,10},{10,12},{12,14},{14,16},{16,18},{18... | collective-permute-start | bytes 811016 | tf_op jit(solution)/shard_map/ppermute | solution.py:172
  47.5 8.4 %copy-start.3 = (bf16[512,1024]{1,0:T(8,128)(2,1)S(1)}, bf16[512,1024]{1,0:T(8,128)(2,1)}, u32[]{:S(2)}) copy-start(bf16[512,1024]{1,0:T(8,128)(2,1)} %get-tuple-element.26.values_ref) | copy-start | bytes 3145732
  49.7 9.1 %collective-permute-start.1 = (s16[528,256]{1,0:T(8,128)(2,1)S(1)}, s16[528,256]{1,0:T(8,128)(2,1)S(1)}, u32[]{:S(2)}, u32[]{:S(2)}) collective-permute-start(s16[528,256]{1,0:T(8,128)(2,1)S(1)} %get-tuple-element.25), channel_id=1, source_target_pairs={{0,2},{2,4},{4,6},{6,8},{8,10},{10,12},{12,14},{14,16},{16,18},{18... | collective-permute-start | bytes 811016 | tf_op jit(solution)/shard_map/ppermute | solution.py:172
  58.1 8.6 %collective-permute-start.4 = (s16[528,256]{1,0:T(8,128)(2,1)S(1)}, s16[528,256]{1,0:T(8,128)(2,1)S(1)}, u32[]{:S(2)}, u32[]{:S(2)}) collective-permute-start(s16[528,256]{1,0:T(8,128)(2,1)S(1)} %get-tuple-element.32), channel_id=1, source_target_pairs={{0,2},{2,4},{4,6},{6,8},{8,10},{10,12},{12,14},{14,16},{16,18},{18... | collective-permute-start | bytes 811016 | tf_op jit(solution)/shard_map/ppermute | solution.py:172
  58.8 7.9 %copy-start.2 = (bf16[512,1024]{1,0:T(8,128)(2,1)S(1)}, bf16[512,1024]{1,0:T(8,128)(2,1)}, u32[]{:S(2)}) copy-start(bf16[512,1024]{1,0:T(8,128)(2,1)} %get-tuple-element.31.values_ref) | copy-start | bytes 3145732
  61.0 8.8 %collective-permute-start.3 = (s16[528,256]{1,0:T(8,128)(2,1)S(1)}, s16[528,256]{1,0:T(8,128)(2,1)S(1)}, u32[]{:S(2)}, u32[]{:S(2)}) collective-permute-start(s16[528,256]{1,0:T(8,128)(2,1)S(1)} %get-tuple-element.30), channel_id=1, source_target_pairs={{0,2},{2,4},{4,6},{6,8},{8,10},{10,12},{12,14},{14,16},{16,18},{18... | collective-permute-start | bytes 811016 | tf_op jit(solution)/shard_map/ppermute | solution.py:172
  68.9 8.6 %collective-permute-start.6 = (s16[528,256]{1,0:T(8,128)(2,1)S(1)}, s16[528,256]{1,0:T(8,128)(2,1)S(1)}, u32[]{:S(2)}, u32[]{:S(2)}) collective-permute-start(s16[528,256]{1,0:T(8,128)(2,1)S(1)} %get-tuple-element.37), channel_id=1, source_target_pairs={{0,2},{2,4},{4,6},{6,8},{8,10},{10,12},{12,14},{14,16},{16,18},{18... | collective-permute-start | bytes 811016 | tf_op jit(solution)/shard_map/ppermute | solution.py:172
  69.8 7.7 %copy-start.1 = (bf16[512,1024]{1,0:T(8,128)(2,1)S(1)}, bf16[512,1024]{1,0:T(8,128)(2,1)}, u32[]{:S(2)}) copy-start(bf16[512,1024]{1,0:T(8,128)(2,1)} %get-tuple-element.36.values_ref) | copy-start | bytes 3145732
  72.0 8.6 %collective-permute-start.5 = (s16[528,256]{1,0:T(8,128)(2,1)S(1)}, s16[528,256]{1,0:T(8,128)(2,1)S(1)}, u32[]{:S(2)}, u32[]{:S(2)}) collective-permute-start(s16[528,256]{1,0:T(8,128)(2,1)S(1)} %get-tuple-element.35), channel_id=1, source_target_pairs={{0,2},{2,4},{4,6},{6,8},{8,10},{10,12},{12,14},{14,16},{16,18},{18... | collective-permute-start | bytes 811016 | tf_op jit(solution)/shard_map/ppermute | solution.py:172
